TPU v7x, 32 devices: a whole 2x2x4 slice. The times are simulated.
32 devices in a mesh: seq: 8 (over z, x), fsdp: 4 (over y, core).
Axes of the slice: x: 2, y: 2, z: 4, core: 2. Of those that a mesh axis runs over, the one named last changes fastest.
Arguments:
- tokens: bfloat16 [4, 1024, 2048], P('fsdp', 'seq'), may hold values from -6 to 6
- cotangent: bfloat16 [4, 1024, 2048], P('fsdp', 'seq'), may hold values from -6 to 6
- routes: int32 [4, 1024, 8], P('fsdp', 'seq'), may hold values from 0 to 63, all different within a row; in each aligned block of 128 rows (0 to 127, 128 to 255, ..., all dimensions but the last counted through in order) at most 32 rows name the same one
- norm1_gain: bfloat16 [2048], P(('seq', 'fsdp')), may hold values from 0.099609375 to 1.8984375
- query_weight: bfloat16 [2048, 2048], P(('seq', 'fsdp')), may hold values from -0.125 to 0.125
- key_weight: bfloat16 [2048, 2048], P(('seq', 'fsdp')), may hold values from -0.125 to 0.125
- value_weight: bfloat16 [2048, 2048], P(('seq', 'fsdp')), may hold values from -0.125 to 0.125
- output_weight: bfloat16 [2048, 2048], P(('seq', 'fsdp')), may hold values from -2 to 2
- norm2_gain: bfloat16 [2048], P(('seq', 'fsdp')), may hold values from 0.099609375 to 1.8984375
- router_weight: bfloat16 [2048, 64], P(('seq', 'fsdp')), may hold values from -0.125 to 0.125
- expert_gate: bfloat16 [128, 2048, 512], P(('seq', 'fsdp')), may hold values from -0.125 to 0.125
- expert_up: bfloat16 [128, 2048, 512], P(('seq', 'fsdp')), may hold values from -0.125 to 0.125
- expert_down: bfloat16 [128, 512, 2048], P(('seq', 'fsdp')), may hold values from -0.75 to 0.75
Outputs:
- block_out: bfloat16 [4, 1024, 2048], P('fsdp', 'seq')
- input_grad: float32 [4, 1024, 2048], P('fsdp', 'seq')
- norm1_gain_grad: float32 [2048], P(('seq', 'fsdp'))
- query_weight_grad: float32 [2048, 2048], P(('seq', 'fsdp'))
- key_weight_grad: float32 [2048, 2048], P(('seq', 'fsdp'))
- value_weight_grad: float32 [2048, 2048], P(('seq', 'fsdp'))
- output_weight_grad: float32 [2048, 2048], P(('seq', 'fsdp'))
- norm2_gain_grad: float32 [2048], P(('seq', 'fsdp'))
- router_weight_grad: float32 [2048, 64], P(('seq', 'fsdp'))
- expert_gate_grad: float32 [128, 2048, 512], P(('seq', 'fsdp'))
- expert_up_grad: float32 [128, 2048, 512], P(('seq', 'fsdp'))
- expert_down_grad: float32 [128, 512, 2048], P(('seq', 'fsdp'))
Inputs may be any that keep to these rules, and one draw needn't show every extreme that they name: `routes`: each row names 8 different experts. Among the 128 rows of one device (aligned blocks of the flattened sequences) no expert is named more than 32 times, and in every draw some expert is named exactly 32 times in some block; every expert is named somewhere.
All inputs are finite; a program needn't handle non-finite values.
Results may differ from a plain program's by a relative error of at most 0.02.
Values may be sent and summed in bfloat16 or wider, within the bound.
A program may use at most 448 MiB of HBM per device.

v0:
```python
import jax
import jax.numpy as jnp
from jax import lax
from jax.sharding import PartitionSpec as P

H = 16
HD = 128
SPLIT = 2
AXES = ("seq", "fsdp")
epsilon = 1e-06
rope_base = 50000.0
bf16 = jnp.bfloat16
f32 = jnp.float32


def norm_rows(values, scales):
    mean_sq = jnp.mean(values * values, axis=-1, keepdims=True)
    return values * lax.rsqrt(mean_sq + epsilon) * scales


def rope_tables(positions, head_dim):
    half_dim = head_dim // 2
    frequency = rope_base ** (-(2.0 * jnp.arange(half_dim, dtype=f32)) / head_dim)
    angles = positions.astype(f32)[:, None] * frequency[None, :]
    return (jnp.cos(angles), jnp.sin(angles))


def rotate(values, cosine, sine_tab, inverse):
    half_dim = values.shape[-1] // 2
    low_half = values[..., :half_dim]
    high_half = values[..., half_dim:]
    cos_rows = cosine[:, None, :]
    sin_rows = -sine_tab[:, None, :] if inverse else sine_tab[:, None, :]
    return jnp.concatenate(
        [low_half * cos_rows - high_half * sin_rows, high_half * cos_rows + low_half * sin_rows],
        axis=-1,
    )


def route_weights(logits, chosen):
    expo = jnp.exp(logits)
    probability = expo / jnp.sum(expo, axis=-1, keepdims=True)
    experts = jnp.arange(logits.shape[1], dtype=jnp.int32)
    match = (chosen[:, :, None] == experts).astype(f32)
    picked = jnp.sum(match * probability[:, None, :], axis=-1)
    return picked / jnp.sum(picked, axis=-1, keepdims=True)


def mm(left, right):
    return jnp.dot(left, right, preferred_element_type=f32)


def mm_tn(left, right):
    return lax.dot_general(left, right, (((0,), (0,)), ((), ())), preferred_element_type=f32)


def mm_nt(left, right):
    return lax.dot_general(left, right, (((1,), (1,)), ((), ())), preferred_element_type=f32)


def ein(spec, *args):
    return jnp.einsum(spec, *args, preferred_element_type=f32)


def body(
    tokens,
    cotangent,
    routes,
    norm1_gain,
    query_weight,
    key_weight,
    value_weight,
    output_weight,
    norm2_gain,
    router_weight,
    expert_gate,
    expert_up,
    expert_down,
):
    n_seq = lax.axis_size("seq")
    n_fsdp = lax.axis_size("fsdp")
    n_dev = n_seq * n_fsdp
    seq_at = lax.axis_index("seq")
    dev_at = seq_at * n_fsdp + lax.axis_index("fsdp")
    tok_rows, width = (tokens.shape[1], tokens.shape[2])
    length = tok_rows * n_seq
    heads = H // n_seq
    cols = heads * HD
    shard = query_weight.shape[0]
    experts = router_weight.shape[1]
    top_k = routes.shape[2]
    capacity = tok_rows * top_k // experts * 2
    pieces = expert_gate.shape[0]
    n_loc = max(1, pieces // SPLIT)
    per_loc = pieces // n_loc
    first_expert = dev_at * pieces // SPLIT
    x_own = tokens[0]
    cot_own = cotangent[0]
    chosen = routes[0]
    routes_all = lax.all_gather(chosen, AXES, axis=0, tiled=True)
    x_seq = lax.all_gather(x_own, "seq", axis=0, tiled=True)
    small = jnp.concatenate(
        [
            router_weight,
            norm1_gain[:, None],
            norm2_gain[:, None],
            jnp.zeros((shard, 128 - experts - 2), bf16),
        ],
        axis=1,
    )
    blocks = jnp.concatenate(
        [
            query_weight.reshape(shard, n_seq, cols),
            key_weight.reshape(shard, n_seq, cols),
            value_weight.reshape(shard, n_seq, cols),
            jnp.broadcast_to(small[:, None, :], (shard, n_seq, 128)),
        ],
        axis=2,
    ).transpose(1, 0, 2)
    moved = lax.all_to_all(blocks, "seq", split_axis=0, concat_axis=0, tiled=True)
    packed = lax.all_gather(moved, "fsdp", axis=1).reshape(width, 3 * cols + 128)
    w_qkv = packed[:, : 3 * cols]
    router_full = packed[:, 3 * cols : 3 * cols + experts]
    gain_in = packed[:, 3 * cols + experts].astype(f32)
    gain_mid = packed[:, 3 * cols + experts + 1].astype(f32)
    out_full = lax.all_gather(output_weight, AXES, axis=0, tiled=True)
    out_rows = lax.dynamic_slice_in_dim(out_full, seq_at * cols, cols, 0)
    cot_all = lax.all_gather(cot_own, AXES, axis=0, tiled=True)
    cosine, sine_tab = rope_tables(jnp.arange(length, dtype=jnp.int32), HD)
    normed_in = norm_rows(x_seq.astype(f32), gain_in).astype(bf16)
    qkv = mm(normed_in, w_qkv)
    q = rotate(qkv[:, :cols].reshape(length, heads, HD), cosine, sine_tab, False).astype(bf16)
    k = rotate(qkv[:, cols : 2 * cols].reshape(length, heads, HD), cosine, sine_tab, False).astype(
        bf16
    )
    v = qkv[:, 2 * cols :].astype(bf16).reshape(length, heads, HD)
    scale = HD ** (-0.5)
    scores = ein("qhd,khd->hqk", q, k) * scale
    totals = jnp.log(jnp.sum(jnp.exp(scores), axis=-1))
    probs = jnp.exp(scores - totals[..., None])
    attn_heads = ein("hqk,khd->qhd", probs.astype(bf16), v).astype(bf16)
    attn_flat = attn_heads.reshape(length, cols)
    attn_rows = lax.all_to_all(attn_flat, "seq", split_axis=0, concat_axis=1, tiled=True)
    x_own32 = x_own.astype(f32)
    residual = x_own32 + mm(attn_rows, out_full)
    normed_mid = norm_rows(residual, gain_mid).astype(bf16)
    x_all = lax.all_gather(normed_mid, AXES, axis=0, tiled=True)
    logits_all = mm(x_all, router_full)
    w_all = route_weights(logits_all, routes_all)
    local = first_expert + jnp.arange(n_loc, dtype=jnp.int32)
    match = routes_all.reshape(n_dev, tok_rows, top_k)[:, None] == local[None, :, None, None]
    hit = jnp.any(match, axis=-1)
    w_hit = jnp.sum(jnp.where(match, w_all.reshape(n_dev, 1, tok_rows, top_k), 0.0), axis=-1)
    tri = (jnp.arange(tok_rows)[:, None] <= jnp.arange(tok_rows)[None, :]).astype(bf16)
    place = ein("bet,tu->beu", hit.astype(bf16), tri).astype(jnp.int32) - 1
    slots = jnp.arange(capacity, dtype=jnp.int32)
    pick = hit[:, :, None, :] & (place[:, :, None, :] == slots[None, None, :, None])
    one = pick.astype(bf16)
    w_slot = jnp.sum(jnp.where(pick, w_hit[:, :, None, :], 0.0), axis=-1)
    rows_of = lambda a: ein("best,btd->ebsd", one, a.reshape(n_dev, tok_rows, width)).reshape(
        n_loc, n_dev * capacity, width
    )
    rows_in = rows_of(x_all).astype(bf16)
    rows_cot = rows_of(cot_all)
    w_rows = w_slot.transpose(1, 0, 2).reshape(n_loc, n_dev * capacity, 1)
    rows_grad = (w_rows * rows_cot).astype(bf16)
    gate = expert_gate.reshape(n_loc, per_loc, width, -1)
    up = expert_up.reshape(n_loc, per_loc, width, -1)
    down = expert_down.reshape(n_loc, per_loc, -1, width)
    pre_gate = ein("erd,epdf->eprf", rows_in, gate)
    pre_up = ein("erd,epdf->eprf", rows_in, up)
    sig = jax.nn.sigmoid(pre_gate)
    active = pre_gate * sig
    hidden = (active * pre_up).astype(bf16)
    hidden_grad = ein("erd,epfd->eprf", rows_grad, down)
    gate_grad = (hidden_grad * pre_up * sig * (1.0 + pre_gate * (1.0 - sig))).astype(bf16)
    up_grad = (hidden_grad * active).astype(bf16)
    back = ein("eprf,epdf->erd", gate_grad, gate) + ein("eprf,epdf->erd", up_grad, up)
    out = ein("eprf,epfd->erd", hidden, down)
    w_back = jnp.sum(rows_cot * out, axis=-1)
    spread = (
        lambda a: ein("best,ebsd->btd", one, a.astype(bf16).reshape(n_loc, n_dev, capacity, width))
        .astype(bf16)
        .reshape(n_dev * tok_rows, width)
    )
    back_own = lax.psum_scatter(spread(back), AXES, scatter_dimension=0, tiled=True)
    w_tok = jnp.sum(
        jnp.where(pick, w_back.reshape(n_loc, n_dev, capacity).transpose(1, 0, 2)[..., None], 0.0),
        axis=2,
    )
    w_parts = lax.all_to_all(w_tok, AXES, split_axis=0, concat_axis=0, tiled=True)
    w_by_expert = w_parts.reshape(experts, n_dev * n_loc // experts, tok_rows).sum(axis=1)
    own_match = (chosen[:, :, None] == jnp.arange(experts, dtype=jnp.int32)).astype(f32)
    weight_grad = jnp.sum(own_match * w_by_expert.T[:, None, :], axis=-1)
    moe_own = lax.psum_scatter(spread(w_rows * out), AXES, scatter_dimension=0, tiled=True)
    block_out = (residual + moe_own.astype(f32)).astype(bf16)
    down_grad = ein("eprf,erd->epfd", hidden, rows_grad).reshape(expert_down.shape)
    gate_weight_grad = ein("erd,eprf->epdf", rows_in, gate_grad).reshape(expert_gate.shape)
    up_weight_grad = ein("erd,eprf->epdf", rows_in, up_grad).reshape(expert_up.shape)
    logits = mm(normed_mid, router_full)
    _, route_back = jax.vjp(lambda values: route_weights(values, chosen), logits)
    logit_grad = route_back(weight_grad)[0].astype(bf16)
    normed_total = back_own.astype(f32) + mm_nt(logit_grad, router_full)
    logit_all = lax.all_gather(logit_grad, AXES, axis=0, tiled=True)
    x_cols = lax.dynamic_slice_in_dim(x_all, dev_at * shard, shard, 1)
    grad_router = mm_tn(x_cols, logit_all)
    cot32 = cot_own.astype(f32)
    _, norm_back = jax.vjp(norm_rows, residual, gain_mid)
    resid_part, gain_two = norm_back(normed_total)
    resid_grad = cot32 + resid_part
    resid_seq = lax.all_gather(resid_grad.astype(bf16), "seq", axis=0, tiled=True)
    grad_out_rows = mm_tn(attn_flat, resid_seq)
    grad_output = lax.psum_scatter(grad_out_rows, "fsdp", scatter_dimension=0, tiled=True)
    attn_grad = mm_nt(resid_seq, out_rows).astype(bf16).reshape(length, heads, HD)
    delta = jnp.sum(attn_grad.astype(f32) * attn_heads.astype(f32), axis=-1)
    v_grad = ein("hqk,qhd->khd", probs.astype(bf16), attn_grad).astype(bf16)
    p_grad = ein("qhd,khd->hqk", attn_grad, v)
    s_grad = (probs * (p_grad - delta.T[:, :, None]) * scale).astype(bf16)
    q_grad = ein("hqk,khd->qhd", s_grad, k).astype(bf16)
    k_grad = ein("hqk,qhd->khd", s_grad, q).astype(bf16)
    q_rows = rotate(q_grad.astype(f32), cosine, sine_tab, True).astype(bf16)
    k_rows = rotate(k_grad.astype(f32), cosine, sine_tab, True).astype(bf16)
    d_qkv = jnp.concatenate([a.reshape(length, cols) for a in (q_rows, k_rows, v_grad)], axis=1)
    in_part = mm_nt(d_qkv, w_qkv).astype(bf16)
    normed_in_grad = lax.psum_scatter(in_part, "seq", scatter_dimension=0, tiled=True).astype(f32)
    _, norm_back_in = jax.vjp(norm_rows, x_own32, gain_in)
    input_part, gain_one = norm_back_in(normed_in_grad)
    input_grad = resid_grad + input_part
    grad_qkv = mm_tn(normed_in, d_qkv).reshape(n_seq, n_fsdp, shard, 3 * cols)
    grad_qkv = lax.psum_scatter(grad_qkv, "fsdp", scatter_dimension=1, tiled=False)
    grad_qkv = lax.all_to_all(grad_qkv, "seq", split_axis=0, concat_axis=0, tiled=True)
    grad_qkv = (
        grad_qkv.reshape(n_seq, shard, 3, cols).transpose(2, 1, 0, 3).reshape(3, shard, width)
    )
    gains = lax.psum_scatter(
        jnp.stack([gain_one, gain_two]).reshape(2, n_dev, shard),
        AXES,
        scatter_dimension=1,
        tiled=False,
    )
    return (
        block_out[None],
        input_grad[None],
        gains[0],
        grad_qkv[0],
        grad_qkv[1],
        grad_qkv[2],
        grad_output,
        gains[1],
        grad_router,
        gate_weight_grad,
        up_weight_grad,
        down_grad,
    )


def solution(mesh):
    rows3 = P("fsdp", "seq", None)
    flat = P(AXES)
    two = P(AXES, None)
    three = P(AXES, None, None)
    return jax.shard_map(
        body,
        mesh=mesh,
        in_specs=(rows3, rows3, rows3, flat, two, two, two, two, flat, two, three, three, three),
        out_specs=(rows3, rows3, flat, two, two, two, two, flat, two, three, three, three),
        check_vma=False,
    )
```

profile of v0, /device:TPU:0, one launch (start us, length us, event | category | flops | bytes accessed | tf_op | source)
XLA Modules:
  0.0 1324.9 jit_solution(16863959521056442889)
XLA Ops:
  12.9 30.4 %all_to_all.34 = bf16[8,64,896]{2,1,0:T(8,128)(2,1)S(1)} all-to-all(bf16[8,64,896]{2,1,0:T(8,128)(2,1)S(1)} %copy.233), channel_id=1, replica_groups=mesh['seq'=8,'fsdp'=4] {'seq'}, dimensions={0} | all-to-all | bytes 1835008 | tf_op jit(solution)/shard_map/all_to_all | solution.py:120
  46.9 3.1 fusion.80
  50.0 25.2 %all-gather.19.cloned.1.call-done = bf16[8,256,896]{2,0,1:T(8,128)(2,1)} async-done(((bf16[8,64,896]{2,0,1:T(8,128)(2,1)}), bf16[8,256,896]{2,0,1:T(8,128)(2,1)}) %all-gather.19.cloned.1.call-update) | async-done | bytes 3670032 | tf_op jit(solution)/shard_map/all_gather | solution.py:121
  80.2 69.8 %all-gather.17.cloned.1.call-done = bf16[1,1024,2048]{2,1,0:T(8,128)(2,1)} async-done(((bf16[1,128,2048]{2,1,0:T(8,128)(2,1)}), bf16[1,1024,2048]{2,1,0:T(8,128)(2,1)}) %all-gather.17.cloned.1.call-update) | async-done | bytes 4194320 | tf_op jit(solution)/shard_map/all_gather | solution.py:101
  150.0 3.1 fusion.5
  153.7 6.6 fusion.30
  171.2 3.4 subtract_convert_fusion.3
  174.6 9.4 fusion.8
  184.1 4.2 fusion.36
  189.1 28.2 %all_to_all.35 = bf16[8,128,256]{1,2,0:T(8,128)(2,1)S(1)} all-to-all(bf16[8,128,256]{1,2,0:T(8,128)(2,1)S(1)} %copy.241), channel_id=1, replica_groups=mesh['seq'=8,'fsdp'=4] {'seq'}, dimensions={0} | all-to-all | bytes 1048576 | tf_op jit(solution)/shard_map/all_to_all | solution.py:143
  217.3 14.1 %all-gather.11.cloned.1.call-done = bf16[2048,2048]{1,0:T(8,128)(2,1)} async-done(((bf16[64,2048]{1,0:T(8,128)(2,1)}), bf16[2048,2048]{1,0:T(8,128)(2,1)}) %all-gather.11.cloned.1.call-update) | async-done | bytes 8388624 | tf_op jit(solution)/shard_map/all_gather | solution.py:126
  231.4 4.8 multiply_reduce_fusion.3
  238.2 40.8 %all-gather.2 = s32[1,4096,8]{1,2,0:T(8,128)S(1)} all-gather(s32[1,128,8]{1,2,0:T(8,128)S(1)} %copy-done.24), channel_id=4, replica_groups=mesh['seq'=8,'fsdp'=4] {'seq','fsdp'}, dimensions={1}, use_global_device_ids=true | all-gather | bytes 135168 | tf_op jit(solution)/shard_map/all_gather | solution.py:100
  279.3 68.4 %all-gather.21.cloned.1.call-done = bf16[1,4096,2048]{2,1,0:T(8,128)(2,1)} async-done(((bf16[1,128,2048]{2,1,0:T(8,128)(2,1)}), bf16[1,4096,2048]{2,1,0:T(8,128)(2,1)}) %all-gather.21.cloned.1.call-update) | async-done | bytes 16777232 | tf_op jit(solution)/shard_map/all_gather | solution.py:128
  347.7 7.0 convolution_bitcast_fusion
  354.8 6.2 copy.247
  361.0 102.1 %all-gather.13.cloned.1.call-done = bf16[4096,2048]{1,0:T(8,128)(2,1)} async-done(((bf16[128,2048]{1,0:T(8,128)(2,1)}), bf16[4096,2048]{1,0:T(8,128)(2,1)}) %all-gather.13.cloned.1.call-update) | async-done | bytes 16777232 | tf_op jit(solution)/shard_map/all_gather | solution.py:147
  463.0 9.4 convert_bitcast_fusion
  472.4 8.3 copy.245
  480.7 15.8 %fusion.98 = f32[2,1024,2,512]{3,1,2,0:T(8,128)} fusion(bf16[2,1024,2048,1]{2,1,3,0:T(8,128)(2,1)} %bitcast.248, bf16[2,2,2048,512]{3,2,1,0:T(8,128)(2,1)} %bitcast.297), kind=kOutput, calls=%fused_computation.181 | convolution fusion | flops 8589934592 | bytes 25165824 | tf_op jit(solution)/shard_map/erd,epdf->eprf/dot_general | solution.py:62
  496.4 15.0 %fusion.17 = (bf16[2,2,1024,512]{3,2,1,0:T(8,128)(2,1)S(1)}, f32[2,1024,2,512]{3,1,2,0:T(8,128)}) fusion(f32[2,1024,2,512]{3,1,2,0:T(8,128)} %fusion.98, bf16[2,1024,2048,1]{2,1,3,0:T(8,128)(2,1)S(1)} %bitcast.251, bf16[2,2,2048,512]{3,2,1,0:T(8,128)(2,1)} %bitcast.299), kind=kOutput, calls=%fused_computation.31 | convolution fusion | flops 8602517504 | bytes 37748736 | tf_op jit(solution)/shard_map/erd,epdf->eprf/dot_general | solution.py:62
  511.4 19.9 %fusion.3 = (f32[2,1024]{1,0:T(2,128)S(1)}, f32[2,1024,2048,1]{2,1,3,0:T(8,128)}) fusion(f32[2,32,32,2048]{3,2,1,0:T(8,128)} %copy.247, bf16[2,2,1024,512]{3,2,1,0:T(8,128)(2,1)S(1)} %get-tuple-element.133, bf16[2,2,512,2048]{3,2,1,0:T(8,128)(2,1)} %bitcast.295), kind=kOutput, calls=%fused_computation.8 | convolution fusion | flops 8598321152 | bytes 46145536 | tf_op jit(solution)/shard_map/eprf,epfd->erd/dot_general | solution.py:62
  531.4 11.0 fusion.97
  545.6 17.0 %fusion.2 = (bf16[2,1024,2048]{2,1,0:T(8,128)(2,1)}, bf16[2,1024,2048]{2,1,0:T(8,128)(2,1)}) fusion(f32[2,32,32,2048]{3,2,1,0:T(8,128)} %copy.247, f32[2,1024]{1,0:T(2,128)S(1)} %mul.567, f32[2,1024,2048,1]{2,1,3,0:T(8,128)} %get-tuple-element.136), kind=kLoop, calls=%fused_computation.7 | loop fusion | flops 16777216 | bytes 50339840 | tf_op jit(solution)/shard_map/convert_element_type | solution.py:166
  562.6 18.9 %fusion.16 = (bf16[2,2,1024,512]{3,2,1,0:T(8,128)(2,1)}, bf16[2,2,1024,512]{3,2,1,0:T(8,128)(2,1)S(1)}) fusion(f32[2,1024,2,512]{3,1,2,0:T(8,128)} %fusion.98, f32[2,1024,2,512]{3,1,2,0:T(8,128)} %get-tuple-element.134, bf16[2,2,512,2048]{3,2,1,0:T(8,128)(2,1)} %bitcast.296, bf16[2,1024,2048]{2,1,0:T(8,128)(2,1)} %get-tuple-element.122), kind=kOutput, calls=%fused_computation.29 | convolution fusion | flops 8617197568 | bytes 41943040 | tf_op jit(solution)/shard_map/erd,epfd->eprf/dot_general | solution.py:62
  581.5 16.2 %fusion.99 = f32[2,1024,2048,1]{2,1,3,0:T(8,128)} fusion(bf16[2,2,1024,512]{3,2,1,0:T(8,128)(2,1)S(1)} %get-tuple-element.98, bf16[2,2,2048,512]{3,2,1,0:T(8,128)(2,1)} %bitcast.298), kind=kOutput, calls=%fused_computation.182 | convolution fusion | flops 8589934592 | bytes 29360128 | tf_op jit(solution)/shard_map/eprf,epdf->erd/dot_general | solution.py:62
  597.6 16.9 %fusion.1 = bf16[2,1024,2048]{2,1,0:T(8,128)(2,1)} fusion(f32[2,1024,2048,1]{2,1,3,0:T(8,128)} %fusion.99, bf16[2,2,1024,512]{3,2,1,0:T(8,128)(2,1)} %get-tuple-element.97, bf16[2,2,2048,512]{3,2,1,0:T(8,128)(2,1)} %bitcast.300), kind=kOutput, calls=%fused_computation.4 | convolution fusion | flops 8598323200 | bytes 37748736 | tf_op jit(solution)/shard_map/eprf,epdf->erd/dot_general | solution.py:62
  614.6 10.7 bitcast_convert_fusion
  630.7 11.0 all-to-all-done.2
  641.9 167.0 %reduce-scatter.8.cloned.1.call-done = bf16[128,2048]{1,0:T(8,128)(2,1)} async-done(((bf16[4096,2048]{1,0:T(8,128)(2,1)}), bf16[128,2048]{1,0:T(8,128)(2,1)}) %reduce-scatter.8.cloned.1.call-update) | async-done | bytes 524304 | tf_op jit(solution)/shard_map/reduce_scatter | solution.py:186
  812.1 74.1 %all-gather.15.cloned.1.call-done = bf16[1024,2048]{1,0:T(8,128)(2,1)} async-done(((bf16[128,2048]{1,0:T(8,128)(2,1)}), bf16[1024,2048]{1,0:T(8,128)(2,1)}) %all-gather.15.cloned.1.call-update) | async-done | bytes 4194320 | tf_op jit(solution)/shard_map/all_gather | solution.py:211
  886.2 4.1 multiply_reduce_fusion.1
  890.3 5.9 fusion.39
  906.2 6.8 fusion.47
  913.0 3.4 copy.262
  916.4 8.0 convolution_convert_fusion
  924.5 11.1 bitcast_convert_fusion.1
  937.0 16.9 %fusion.101 = f32[2,2,512,2048]{3,2,1,0:T(8,128)} fusion(bf16[2,2,1024,512]{3,2,1,0:T(8,128)(2,1)} %copy-done.34, bf16[2,1024,2048,1]{2,1,3,0:T(8,128)(2,1)} %bitcast.249), kind=kOutput, calls=%fused_computation.184 | convolution fusion | flops 8589934592 | bytes 29360128 | tf_op jit(solution)/shard_map/erd,eprf->epdf/dot_general | solution.py:62
  956.6 16.5 %fusion.102 = f32[2,2,512,2048]{3,2,1,0:T(8,128)} fusion(bf16[2,2,1024,512]{3,2,1,0:T(8,128)(2,1)} %get-tuple-element.97, bf16[2,1024,2048,1]{2,1,3,0:T(8,128)(2,1)} %bitcast.250), kind=kOutput, calls=%fused_computation.185 | convolution fusion | flops 8589934592 | bytes 29360128 | tf_op jit(solution)/shard_map/erd,eprf->epdf/dot_general | solution.py:62
  973.9 5.7 all-to-all-start.3
  979.7 16.6 %fusion.9 = f32[2,2,512,2048]{3,2,1,0:T(8,128)} fusion(bf16[2,2,1024,512]{3,2,1,0:T(8,128)(2,1)} %copy-done.33, bf16[2,1024,2048]{2,1,0:T(8,128)(2,1)} %get-tuple-element.122), kind=kOutput, calls=%fused_computation.20 | convolution fusion | flops 8589934592 | bytes 29360128 | tf_op jit(solution)/shard_map/eprf,erd->epfd/dot_general | solution.py:62
  996.3 16.4 %copy.269 = f32[4,2048,512]{2,1,0:T(8,128)} copy(f32[4,2048,512]{1,2,0:T(8,128)} %bitcast.240) | data formatting | bytes 33554432
  1012.6 16.5 %copy.270 = f32[4,2048,512]{2,1,0:T(8,128)} copy(f32[4,2048,512]{1,2,0:T(8,128)} %bitcast.241) | data formatting | bytes 33554432
  1029.1 42.9 %all_gather.35 = bf16[4096,64]{0,1:T(8,128)(2,1)S(1)} all-gather(bf16[128,64]{0,1:T(8,128)(2,1)S(1)} %multiply_convert_fusion.2), channel_id=1, replica_groups=mesh['seq'=8,'fsdp'=4] {'seq','fsdp'}, dimensions={0}, use_global_device_ids=true | all-gather | bytes 540672 | tf_op jit(solution)/shard_map/all_gather | solution.py:204
  1074.6 21.2 %reduce-scatter.10.cloned.1.call-done = bf16[128,2048]{1,0:T(8,128)(2,1)} async-done(((bf16[1024,2048]{1,0:T(8,128)(2,1)}), bf16[128,2048]{1,0:T(8,128)(2,1)}) %reduce-scatter.10.cloned.1.call-update) | async-done | bytes 524304 | tf_op jit(solution)/shard_map/reduce_scatter | solution.py:225
  1097.6 45.8 %all-reduce = f32[2,32,64]{2,0,1:T(2,128)S(1)} all-reduce(f32[2,32,64]{2,0,1:T(2,128)S(1)} %pad_maximum_fusion.7), channel_id=9, replica_groups=mesh['seq'=8,'fsdp'=4] {'seq','fsdp'}, use_global_device_ids=true, to_apply=%region_27.28.clone | all-reduce | flops 4096 | bytes 32768
  1144.0 138.5 %reduce-scatter.6.cloned.1.call-done = bf16[128,2048]{1,0:T(8,128)(2,1)} async-done(((bf16[4096,2048]{1,0:T(8,128)(2,1)}), bf16[128,2048]{1,0:T(8,128)(2,1)}) %reduce-scatter.6.cloned.1.call-update) | async-done | bytes 524304 | tf_op jit(solution)/shard_map/reduce_scatter | solution.py:195
  1293.2 25.0 %reduce-scatter.14.cloned.1.call-done = f32[64,2048]{1,0:T(8,128)} async-done(((f32[256,2048]{1,0:T(8,128)}), f32[64,2048]{1,0:T(8,128)}) %reduce-scatter.14.cloned.1.call-update) | async-done | bytes 524304 | tf_op jit(solution)/shard_map/reduce_scatter | solution.py:213
  (184 shorter events, 71.4 us)
Async XLA Ops:
  7.2 67.9 %all-gather.19.cloned.1.call-start = ((), (), s32[]{:S(2)}) async-start(), calls=%async_computation.18 | async-start | bytes 4587520 | tf_op jit(solution)/shard_map/all_gather | solution.py:121
  44.7 105.3 %all-gather.17.cloned.1.call-start = ((), (), s32[]{:S(2)}) async-start(), calls=%async_computation.17 | async-start | bytes 4718592 | tf_op jit(solution)/shard_map/all_gather | solution.py:101
  45.5 185.9 %all-gather.11.cloned.1.call-start = ((), (), s32[]{:S(2)}) async-start(), calls=%async_computation.9 | async-start | bytes 8650752 | tf_op jit(solution)/shard_map/all_gather | solution.py:126
  46.2 301.5 %all-gather.21.cloned.1.call-start = ((), (), s32[]{:S(2)}) async-start(), calls=%async_computation.19 | async-start | bytes 17301504 | tf_op jit(solution)/shard_map/all_gather | solution.py:128
  46.8 416.2 %all-gather.13.cloned.1.call-start = ((), (), s32[]{:S(2)}) async-start(), calls=%async_computation.10 | async-start | bytes 17301504 | tf_op jit(solution)/shard_map/all_gather | solution.py:147
  49.9 121.3 %copy-start.6 = (f32[1024,64]{1,0:T(8,128)}, f32[1024,64]{1,0:T(8,128)S(1)}, u32[]{:S(2)}) copy-start(f32[1024,64]{1,0:T(8,128)S(1)} %get-tuple-element.126) | copy-start | bytes 786436
  77.7 1.8 copy-start.4
  80.2 72.9 %copy-start.22 = (f32[2048]{0:T(1024)}, f32[2048]{0:T(1024)S(1)}, u32[]{:S(2)}) copy-start(f32[2048]{0:T(1024)S(1)} %get-tuple-element.85) | copy-start | bytes 24580
  80.2 156.0 %copy-start.20 = (f32[2048]{0:T(1024)}, f32[2048]{0:T(1024)S(1)}, u32[]{:S(2)}) copy-start(f32[2048]{0:T(1024)S(1)} %get-tuple-element.84) | copy-start | bytes 24580
  160.4 23.6 %copy-start.10 = (bf16[1024,256]{0,1:T(8,128)(2,1)}, bf16[1024,256]{0,1:T(8,128)(2,1)S(1)}, u32[]{:S(2)}) copy-start(bf16[1024,256]{0,1:T(8,128)(2,1)S(1)} %slice.127) | copy-start | bytes 1572868
  184.0 47.4 %copy-start.2 = (bf16[1,128,2048]{2,1,0:T(8,128)(2,1)S(1)}, bf16[1,128,2048]{2,1,0:T(8,128)(2,1)}, u32[]{:S(2)}) copy-start(bf16[1,128,2048]{2,1,0:T(8,128)(2,1)} %param.13) | copy-start | bytes 1572868
  231.4 6.8 copy-start.24
  236.2 1.0 copy-start
  236.2 42.8 %copy-start.30 = (f32[128]{0:T(128)}, f32[128]{0:T(128)S(1)}, u32[]{:S(2)}) copy-start(f32[128]{0:T(128)S(1)} %get-tuple-element.129) | copy-start | bytes 1540
  236.2 42.8 %copy-start.26 = (f32[128]{0:T(128)}, f32[128]{0:T(128)S(1)}, u32[]{:S(2)}) copy-start(f32[128]{0:T(128)S(1)} %fusion.86) | copy-start | bytes 1540
  238.1 570.7 %reduce-scatter.8.cloned.1.call-start = ((), (), s32[]{:S(2)}) async-start(), calls=%async_computation.12 | async-start | bytes 17301504 | tf_op jit(solution)/shard_map/reduce_scatter | solution.py:186
  480.7 15.8 %copy-start.5 = (bf16[2,32,32,2048]{3,2,1,0:T(8,128)(2,1)S(1)}, bf16[2,32,32,2048]{3,2,1,0:T(8,128)(2,1)}, u32[]{:S(2)}) copy-start(bf16[2,32,32,2048]{3,2,1,0:T(8,128)(2,1)} %copy.245) | copy-start | bytes 25165828
  511.4 19.9 %copy-start.33 = (bf16[2,2,1024,512]{3,2,1,0:T(8,128)(2,1)}, bf16[2,2,1024,512]{3,2,1,0:T(8,128)(2,1)S(1)}, u32[]{:S(2)}) copy-start(bf16[2,2,1024,512]{3,2,1,0:T(8,128)(2,1)S(1)} %get-tuple-element.133) | copy-start | bytes 12582916
  581.5 16.2 %copy-start.34 = (bf16[2,2,1024,512]{3,2,1,0:T(8,128)(2,1)}, bf16[2,2,1024,512]{3,2,1,0:T(8,128)(2,1)S(1)}, u32[]{:S(2)}) copy-start(bf16[2,2,1024,512]{3,2,1,0:T(8,128)(2,1)S(1)} %get-tuple-element.98) | copy-start | bytes 12582916
  625.3 1.0 copy-start.8
  625.3 16.3 %copy-start.25 = (s32[1,128,8]{1,2,0:T(8,128)S(1)}, s32[1,128,8]{1,2,0:T(8,128)}, u32[]{:S(2)}) copy-start(s32[1,128,8]{1,2,0:T(8,128)} %param.15) | copy-start | bytes 12292
  625.3 183.5 %copy-start.1 = (f32[128,2048]{1,0:T(8,128)S(1)}, f32[128,2048]{1,0:T(8,128)}, u32[]{:S(2)}) copy-start(f32[128,2048]{1,0:T(8,128)} %copy-done) | copy-start | bytes 3145732
  625.3 183.5 %copy-start.21 = (f32[2048]{0:T(1024)S(1)}, f32[2048]{0:T(1024)}, u32[]{:S(2)}) copy-start(f32[2048]{0:T(1024)} %copy-done.20) | copy-start | bytes 24580
  625.3 183.5 %copy-start.27 = (f32[128]{0:T(128)S(1)}, f32[128]{0:T(128)}, u32[]{:S(2)}) copy-start(f32[128]{0:T(128)} %copy-done.26) | copy-start | bytes 1540
  625.3 185.3 %copy-start.31 = (f32[128]{0:T(128)S(1)}, f32[128]{0:T(128)}, u32[]{:S(2)}) copy-start(f32[128]{0:T(128)} %copy-done.30) | copy-start | bytes 1540
  625.4 185.3 %copy-start.9 = (bf16[1,128,2048]{2,1,0:T(8,128)(2,1)S(1)}, bf16[1,128,2048]{2,1,0:T(8,128)(2,1)}, u32[]{:S(2)}) copy-start(bf16[1,128,2048]{2,1,0:T(8,128)(2,1)} %param.14) | copy-start | bytes 1572868
  627.8 13.9 %all-to-all-start.2 = ((f32[32,2,128]{2,1,0:T(2,128)}), f32[32,2,128]{2,1,0:T(2,128)S(1)}, u32[]{:S(2)}, u32[]{:S(2)}) async-start(f32[32,2,128]{2,1,0:T(2,128)} %get-tuple-element.92), calls=%async_computation.4 | async-start | bytes 65536 | tf_op jit(solution)/shard_map/all_to_all | solution.py:191
  630.6 255.6 %all-gather.15.cloned.1.call-start = ((), (), s32[]{:S(2)}) async-start(), calls=%async_computation.13 | async-start | bytes 4718592 | tf_op jit(solution)/shard_map/all_gather | solution.py:211
  811.9 162.1 %reduce-scatter.12.cloned.1.call-start = ((), (), s32[]{:S(2)}) async-start(), calls=%async_computation.15 | async-start | bytes 7864320 | tf_op jit(solution)/shard_map/reduce_scatter | solution.py:230
  812.1 84.1 %copy-start.11 = (bf16[1024,256]{0,1:T(8,128)(2,1)S(1)}, bf16[1024,256]{0,1:T(8,128)(2,1)}, u32[]{:S(2)}) copy-start(bf16[1024,256]{0,1:T(8,128)(2,1)} %copy-done.10) | copy-start | bytes 1572868
  886.2 9.9 slice-start
  890.3 5.9 slice-start.1
  896.2 1.4 copy-start.14
  896.2 1.4 copy-start.15
  896.2 3.4 copy-start.12
  896.2 3.4 copy-start.13
  897.6 3.4 copy-start.7
  897.6 3.4 copy-start.16
  899.7 6.6 copy-start.23
  899.7 6.5 copy-start.29
  913.0 3.5 copy-start.19
  916.4 179.5 %reduce-scatter.10.cloned.1.call-start = ((), (), s32[]{:S(2)}) async-start(), calls=%async_computation.14 | async-start | bytes 4718592 | tf_op jit(solution)/shard_map/reduce_scatter | solution.py:225
  924.5 358.0 %reduce-scatter.6.cloned.1.call-start = ((), (), s32[]{:S(2)}) async-start(), calls=%async_computation.11 | async-start | bytes 17301504 | tf_op jit(solution)/shard_map/reduce_scatter | solution.py:195
  935.6 1.2 copy-start.3
  935.6 382.6 %reduce-scatter.14.cloned.1.call-start = ((), (), s32[]{:S(2)}) async-start(), calls=%async_computation.16 | async-start | bytes 2621440 | tf_op jit(solution)/shard_map/reduce_scatter | solution.py:213
  937.0 17.0 %copy-start.18 = (bf16[2,128,1024]{2,1,0:T(8,128)(2,1)S(1)}, bf16[2,128,1024]{2,1,0:T(8,128)(2,1)}, u32[]{:S(2)}) copy-start(bf16[2,128,1024]{2,1,0:T(8,128)(2,1)} %copy-done.17) | copy-start | bytes 1572868
  937.0 17.0 %copy-start.32 = (bf16[1024,2048]{1,0:T(8,128)(2,1)S(1)}, bf16[1024,2048]{1,0:T(8,128)(2,1)}, u32[]{:S(2)}) copy-start(bf16[1024,2048]{1,0:T(8,128)(2,1)} %all-gather.15.cloned.1.call-done) | copy-start | bytes 12582916
  973.9 311.4 %all-to-all-start.3 = ((f32[8,64,768]{2,1,0:T(8,128)}), f32[8,64,768]{2,1,0:T(8,128)}, u32[]{:S(2)}, u32[]{:S(2)}) async-start(f32[8,64,768]{2,1,0:T(8,128)} %bitcast.270), calls=%async_computation.7 | async-start | bytes 3145728 | tf_op jit(solution)/shard_map/all_to_all | solution.py:231
  (2 other events, 1.4 us)
Sparse Core Ops, SparseCore 0:
  44.9 30.1 all-gather.18
  77.2 72.7 all-gather.16
  152.9 78.4 all-gather.10
  234.1 113.5 all-gather.20
  350.5 112.5 all-gather.12
  625.5 183.2 reduce-scatter.7
  812.0 74.2 all-gather.14
  916.5 57.3 reduce-scatter.11
  977.6 118.2 reduce-scatter.9
  1098.0 184.4 reduce-scatter.5
  1285.6 32.5 reduce-scatter.13
where the time goes:
time: 1340 us; the launch traced here: 1320 us
  waiting for transfers between devices  719 us (54%)
  matrix products  265 us (20%)
  blocking collectives  188 us (14%)
  local copies, waits for them, and re-layouts  88.1 us (7%)
  other arithmetic  40.5 us (3%)
  between operations  14.8 us (1%)
    dot_general x19, matrix products, ein(): return jnp.einsum(spec, *args, preferred_element_type=f32)  206 us
    reduce_scatter x1, waiting for transfers between devices, body(): lax.psum_scatter(spread(back), AXES, scatter_dimension=0, tiled=True)  167 us
    reduce_scatter x1, waiting for transfers between devices, body(): lax.psum_scatter(spread(w_rows * out), AXES, scatter_dimension=0, tiled=T...  139 us
    all_gather x1, waiting for transfers between devices, body(): x_all = lax.all_gather(normed_mid, AXES, axis=0, tiled=True)  102 us
    all_gather x1, waiting for transfers between devices, body(): lax.all_gather(resid_grad.astype(bf16), 'seq', axis=0, tiled=True)  74.1 us
    all_gather x1, waiting for transfers between devices, body(): x_seq = lax.all_gather(x_own, 'seq', axis=0, tiled=True)  69.8 us
    all_gather x1, waiting for transfers between devices, body(): cot_all = lax.all_gather(cot_own, AXES, axis=0, tiled=True)  68.4 us
    unnamed x88, local copies, waits for them, and re-layouts  51 us
  transfers between devices with their start and end apart: 13, of which 12 were waited for; matrix products, arithmetic and copies ran while one was open for 14% of the time, Pallas kernels for 0%

commit v1 on v0

--- a/solution.py
+++ b/solution.py
@@ -125,7 +125,15 @@
     gain_mid = packed[:, 3 * cols + experts + 1].astype(f32)
     out_full = lax.all_gather(output_weight, AXES, axis=0, tiled=True)
     out_rows = lax.dynamic_slice_in_dim(out_full, seq_at * cols, cols, 0)
-    cot_all = lax.all_gather(cot_own, AXES, axis=0, tiled=True)
+    ways, here = (lax.axis_size(AXES), lax.axis_index(AXES))
+    grown, reach = (cot_own, 1)
+    while reach < ways:
+        theirs = lax.ppermute(grown, AXES, [(d, d ^ reach) for d in range(ways)])
+        mine_first = jnp.concatenate([grown, theirs], axis=0)
+        theirs_first = jnp.concatenate([theirs, grown], axis=0)
+        grown = jnp.where(here & reach == 0, mine_first, theirs_first)
+        reach = 2 * reach
+    cot_all = grown
     cosine, sine_tab = rope_tables(jnp.arange(length, dtype=jnp.int32), HD)
     normed_in = norm_rows(x_seq.astype(f32), gain_in).astype(bf16)
     qkv = mm(normed_in, w_qkv)

time: 1340 us -> 1770 us (1.32)
  blocking collectives: 188 us -> 525 us
  waiting for transfers between devices: 719 us -> 758 us
  other arithmetic: 40.5 us -> 76.5 us
    all_gather x1, blocking collectives: 40.8 us -> 378 us  [body(): routes_all = lax.all_gather(chosen, AXES, axis=0, tiled=True)]
    ppermute x0 -> x5, waiting for transfers between devices: none -> 211 us  [body(): theirs = lax.ppermute(grown, AXES, [(d, d ^ reach) for d in range(ways)])]
    all_gather x1, waiting for transfers between devices: 102 us -> 0.01 us  [body(): x_all = lax.all_gather(normed_mid, AXES, axis=0, tiled=True)]
    all_gather x1 -> x0, waiting for transfers between devices: 68.4 us -> none  [body(): cot_all = lax.all_gather(cot_own, AXES, axis=0, tiled=True)]
    select_n x0 -> x5, other arithmetic: none -> 36.1 us  [body(): grown = jnp.where(here & reach == 0, mine_first, theirs_first)]
  transfers between devices with their start and end apart: 13 -> 17, of which waited for: 12 -> 14; matrix products, arithmetic and copies ran while one was open for 14% -> 13% of each run, Pallas kernels for 0% -> 0%
where the time goes in v1:
time: 1770 us; the launch traced here: 1760 us
  waiting for transfers between devices  758 us (43%)
  blocking collectives  525 us (30%)
  matrix products  269 us (15%)
  local copies, waits for them, and re-layouts  94 us (5%)
  other arithmetic  76.5 us (4%)
  starting transfers between devices  22.7 us (1%)
    all_gather x1, blocking collectives, body(): routes_all = lax.all_gather(chosen, AXES, axis=0, tiled=True)  378 us
    ppermute x5, waiting for transfers between devices, body(): theirs = lax.ppermute(grown, AXES, [(d, d ^ reach) for d in range(ways)])  211 us
    dot_general x19, matrix products, ein(): return jnp.einsum(spec, *args, preferred_element_type=f32)  209 us
    reduce_scatter x1, waiting for transfers between devices, body(): lax.psum_scatter(spread(back), AXES, scatter_dimension=0, tiled=True)  167 us
    reduce_scatter x1, waiting for transfers between devices, body(): lax.psum_scatter(spread(w_rows * out), AXES, scatter_dimension=0, tiled=T...  139 us
    all_gather x1, waiting for transfers between devices, body(): lax.all_gather(resid_grad.astype(bf16), 'seq', axis=0, tiled=True)  73.3 us
    all_gather x1, waiting for transfers between devices, body(): x_seq = lax.all_gather(x_own, 'seq', axis=0, tiled=True)  69.8 us
    unnamed x88, local copies, waits for them, and re-layouts  51.2 us
  transfers between devices with their start and end apart: 17, of which 14 were waited for; matrix products, arithmetic and copies ran while one was open for 13% of the time, Pallas kernels for 0%

profile of v1, /device:TPU:0, one launch (start us, length us, event | category | flops | bytes accessed | tf_op | source)
XLA Modules:
  0.0 1760.4 jit_solution(9535298972774024231)
XLA Ops:
  12.9 30.4 %all_to_all.34 = bf16[8,64,896]{2,1,0:T(8,128)(2,1)S(1)} all-to-all(bf16[8,64,896]{2,1,0:T(8,128)(2,1)S(1)} %copy.233), channel_id=1, replica_groups=mesh['seq'=8,'fsdp'=4] {'seq'}, dimensions={0} | all-to-all | bytes 1835008 | tf_op jit(solution)/shard_map/all_to_all | solution.py:120
  49.4 25.7 %all-gather.17.cloned.1.call-done = bf16[8,256,896]{2,0,1:T(8,128)(2,1)} async-done(((bf16[8,64,896]{2,0,1:T(8,128)(2,1)}), bf16[8,256,896]{2,0,1:T(8,128)(2,1)}) %all-gather.17.cloned.1.call-update) | async-done | bytes 3670032 | tf_op jit(solution)/shard_map/all_gather | solution.py:121
  80.3 69.8 %all-gather.15.cloned.1.call-done = bf16[1,1024,2048]{2,1,0:T(8,128)(2,1)} async-done(((bf16[1,128,2048]{2,1,0:T(8,128)(2,1)}), bf16[1,1024,2048]{2,1,0:T(8,128)(2,1)}) %all-gather.15.cloned.1.call-update) | async-done | bytes 4194320 | tf_op jit(solution)/shard_map/all_gather | solution.py:101
  153.7 6.6 fusion.30
  174.6 9.4 fusion.8
  184.0 4.2 fusion.36
  189.1 28.4 %all_to_all.35 = bf16[8,128,256]{1,2,0:T(8,128)(2,1)S(1)} all-to-all(bf16[8,128,256]{1,2,0:T(8,128)(2,1)S(1)} %copy.241), channel_id=1, replica_groups=mesh['seq'=8,'fsdp'=4] {'seq'}, dimensions={0} | all-to-all | bytes 1048576 | tf_op jit(solution)/shard_map/all_to_all | solution.py:151
  217.5 14.1 all-gather.9.cloned.1.call-done
  231.6 4.8 multiply_reduce_fusion.3
  242.1 27.8 %collective-permute-done.1 = bf16[256,2048]{1,0:T(8,128)(2,1)} collective-permute-done((bf16[256,2048]{1,0:T(8,128)(2,1)S(1)}, bf16[256,2048]{1,0:T(8,128)(2,1)}, u32[]{:S(2)}, u32[]{:S(2)}) %collective-permute-start.1) | collective-permute-done | bytes 1048608 | tf_op jit(solution)/shard_map/ppermute | solution.py:131
  273.9 72.1 %collective-permute-done.2 = bf16[512,2048]{1,0:T(8,128)(2,1)} collective-permute-done((bf16[512,2048]{1,0:T(8,128)(2,1)S(1)}, bf16[512,2048]{1,0:T(8,128)(2,1)}, u32[]{:S(2)}, u32[]{:S(2)}) %collective-permute-start.2) | collective-permute-done | bytes 2097184 | tf_op jit(solution)/shard_map/ppermute | solution.py:131
  346.0 5.1 maximum_select_fusion.2
  352.8 109.6 %collective-permute-done.3 = bf16[1024,2048]{1,0:T(8,128)(2,1)} collective-permute-done((bf16[1024,2048]{1,0:T(8,128)(2,1)}, bf16[1024,2048]{1,0:T(8,128)(2,1)}, u32[]{:S(2)}, u32[]{:S(2)}) %collective-permute-start.3) | collective-permute-done | bytes 4194336 | tf_op jit(solution)/shard_map/ppermute | solution.py:131
  462.4 9.9 maximum_select_fusion.1
  474.3 378.2 %all-gather.2 = s32[1,4096,8]{1,2,0:T(8,128)S(1)} all-gather(s32[1,128,8]{1,2,0:T(8,128)S(1)} %copy-done.25), channel_id=4, replica_groups=mesh['seq'=8,'fsdp'=4] {'seq','fsdp'}, dimensions={1}, use_global_device_ids=true | all-gather | bytes 135168 | tf_op jit(solution)/shard_map/all_gather | solution.py:100
  852.8 18.5 %maximum_select_fusion = bf16[4096,2048]{1,0:T(8,128)(2,1)} fusion(bf16[2048,2048]{1,0:T(8,128)(2,1)} %collective-permute-done.4, bf16[2048,2048]{1,0:T(8,128)(2,1)} %maximum_select_fusion.1, pred[]{:T(512)S(6)} %eq.86), kind=kLoop, calls=%fused_computation.3 | loop fusion | flops 75497472 | bytes 33554432 | tf_op jit(solution)/shard_map/jit(_where)/select_n | solution.py:134
  871.3 10.8 convolution_bitcast_fusion
  882.1 11.8 copy.247
  893.9 9.4 convert_bitcast_fusion
  903.3 8.3 copy.245
  911.5 15.8 fusion.98
  927.3 15.9 fusion.17
  943.1 19.2 %fusion.3 = (f32[2,1024]{1,0:T(2,128)S(1)}, f32[2,1024,2048,1]{2,1,3,0:T(8,128)}) fusion(f32[2,32,32,2048]{3,2,1,0:T(8,128)} %copy.247, bf16[2,2,1024,512]{3,2,1,0:T(8,128)(2,1)} %get-tuple-element.133, bf16[2,2,512,2048]{3,2,1,0:T(8,128)(2,1)} %bitcast.296), kind=kOutput, calls=%fused_computation.9 | convolution fusion | flops 8598321152 | bytes 46145536 | tf_op jit(solution)/shard_map/eprf,epfd->erd/dot_general | solution.py:62
  962.5 11.0 fusion.97
  976.6 16.9 fusion.2
  993.6 18.7 %fusion.16 = (bf16[2,2,1024,512]{3,2,1,0:T(8,128)(2,1)}, bf16[2,2,1024,512]{3,2,1,0:T(8,128)(2,1)S(1)}) fusion(f32[2,1024,2,512]{3,1,2,0:T(8,128)} %fusion.98, f32[2,1024,2,512]{3,1,2,0:T(8,128)} %get-tuple-element.134, bf16[2,2,512,2048]{3,2,1,0:T(8,128)(2,1)} %bitcast.297, bf16[2,1024,2048]{2,1,0:T(8,128)(2,1)} %get-tuple-element.122), kind=kOutput, calls=%fused_computation.31 | convolution fusion | flops 8617197568 | bytes 41943040 | tf_op jit(solution)/shard_map/erd,epfd->eprf/dot_general | solution.py:62
  1012.3 16.2 fusion.99
  1028.5 16.9 fusion.1
  1045.4 10.7 bitcast_convert_fusion
  1058.6 8.8 all-to-all-start.2
  1067.5 11.0 all-to-all-done.2
  1078.6 166.5 %reduce-scatter.8.cloned.1.call-done = bf16[128,2048]{1,0:T(8,128)(2,1)} async-done(((bf16[4096,2048]{1,0:T(8,128)(2,1)}), bf16[128,2048]{1,0:T(8,128)(2,1)}) %reduce-scatter.8.cloned.1.call-update) | async-done | bytes 524304 | tf_op jit(solution)/shard_map/reduce_scatter | solution.py:194
  1248.7 73.3 %all-gather.13.cloned.1.call-done = bf16[1024,2048]{1,0:T(8,128)(2,1)} async-done(((bf16[128,2048]{1,0:T(8,128)(2,1)}), bf16[1024,2048]{1,0:T(8,128)(2,1)}) %all-gather.13.cloned.1.call-update) | async-done | bytes 4194320 | tf_op jit(solution)/shard_map/all_gather | solution.py:219
  1326.0 5.9 fusion.39
  1341.9 6.7 fusion.47
  1352.1 8.0 convolution_convert_fusion
  1360.2 11.1 bitcast_convert_fusion.1
  1372.7 16.9 fusion.101
  1392.3 16.5 fusion.102
  1409.6 5.8 all-to-all-start.3
  1415.4 16.6 fusion.9
  1432.0 16.4 copy.269
  1448.4 16.4 copy.270
  1464.8 42.8 %all_gather.31 = bf16[4096,64]{0,1:T(8,128)(2,1)S(1)} all-gather(bf16[128,64]{0,1:T(8,128)(2,1)S(1)} %multiply_convert_fusion.2), channel_id=1, replica_groups=mesh['seq'=8,'fsdp'=4] {'seq','fsdp'}, dimensions={0}, use_global_device_ids=true | all-gather | bytes 540672 | tf_op jit(solution)/shard_map/all_gather | solution.py:212
  1510.3 21.3 %reduce-scatter.10.cloned.1.call-done = bf16[128,2048]{1,0:T(8,128)(2,1)} async-done(((bf16[1024,2048]{1,0:T(8,128)(2,1)}), bf16[128,2048]{1,0:T(8,128)(2,1)}) %reduce-scatter.10.cloned.1.call-update) | async-done | bytes 524304 | tf_op jit(solution)/shard_map/reduce_scatter | solution.py:233
  1533.3 45.3 %all-reduce = f32[2,32,64]{2,0,1:T(2,128)S(1)} all-reduce(f32[2,32,64]{2,0,1:T(2,128)S(1)} %pad_maximum_fusion.7), channel_id=8, replica_groups=mesh['seq'=8,'fsdp'=4] {'seq','fsdp'}, use_global_device_ids=true, to_apply=%region_27.28.clone | all-reduce | flops 4096 | bytes 32768
  1579.1 138.6 %reduce-scatter.6.cloned.1.call-done = bf16[128,2048]{1,0:T(8,128)(2,1)} async-done(((bf16[4096,2048]{1,0:T(8,128)(2,1)}), bf16[128,2048]{1,0:T(8,128)(2,1)}) %reduce-scatter.6.cloned.1.call-update) | async-done | bytes 524304 | tf_op jit(solution)/shard_map/reduce_scatter | solution.py:203
  1728.5 24.7 %reduce-scatter.14.cloned.1.call-done = f32[64,2048]{1,0:T(8,128)} async-done(((f32[256,2048]{1,0:T(8,128)}), f32[64,2048]{1,0:T(8,128)}) %reduce-scatter.14.cloned.1.call-update) | async-done | bytes 524304 | tf_op jit(solution)/shard_map/reduce_scatter | solution.py:221
  (196 shorter events, 96.5 us)
Async XLA Ops:
  7.2 67.9 %all-gather.17.cloned.1.call-start = ((), (), s32[]{:S(2)}) async-start(), calls=%async_computation.18 | async-start | bytes 4587520 | tf_op jit(solution)/shard_map/all_gather | solution.py:121
  44.7 105.3 %all-gather.15.cloned.1.call-start = ((), (), s32[]{:S(2)}) async-start(), calls=%async_computation.17 | async-start | bytes 4718592 | tf_op jit(solution)/shard_map/all_gather | solution.py:101
  45.5 186.1 %all-gather.9.cloned.1.call-start = ((), (), s32[]{:S(2)}) async-start(), calls=%async_computation.9 | async-start | bytes 8650752 | tf_op jit(solution)/shard_map/all_gather | solution.py:126
  46.2 847.7 %all-gather.11.cloned.1.call-start = ((), (), s32[]{:S(2)}) async-start(), calls=%async_computation.10 | async-start | bytes 17301504 | tf_op jit(solution)/shard_map/all_gather | solution.py:155
  49.4 121.8 %copy-start.6 = (f32[1024,64]{1,0:T(8,128)}, f32[1024,64]{1,0:T(8,128)S(1)}, u32[]{:S(2)}) copy-start(f32[1024,64]{1,0:T(8,128)S(1)} %get-tuple-element.126) | copy-start | bytes 786436
  77.7 1.8 copy-start.4
  80.3 72.9 %copy-start.23 = (f32[2048]{0:T(1024)}, f32[2048]{0:T(1024)S(1)}, u32[]{:S(2)}) copy-start(f32[2048]{0:T(1024)S(1)} %get-tuple-element.85) | copy-start | bytes 24580
  80.3 156.2 %copy-start.21 = (f32[2048]{0:T(1024)}, f32[2048]{0:T(1024)S(1)}, u32[]{:S(2)}) copy-start(f32[2048]{0:T(1024)S(1)} %get-tuple-element.84) | copy-start | bytes 24580
  160.4 23.6 %copy-start.11 = (bf16[1024,256]{0,1:T(8,128)(2,1)}, bf16[1024,256]{0,1:T(8,128)(2,1)S(1)}, u32[]{:S(2)}) copy-start(bf16[1024,256]{0,1:T(8,128)(2,1)S(1)} %slice.127) | copy-start | bytes 1572868
  184.0 47.6 %copy-start.2 = (bf16[1,128,2048]{2,1,0:T(8,128)(2,1)S(1)}, bf16[1,128,2048]{2,1,0:T(8,128)(2,1)}, u32[]{:S(2)}) copy-start(bf16[1,128,2048]{2,1,0:T(8,128)(2,1)} %param.13) | copy-start | bytes 1572868
  231.6 6.8 copy-start.9
  236.4 5.7 copy-start.31
  236.4 5.7 copy-start.27
  238.3 1006.8 %reduce-scatter.8.cloned.1.call-start = ((), (), s32[]{:S(2)}) async-start(), calls=%async_computation.12 | async-start | bytes 17301504 | tf_op jit(solution)/shard_map/reduce_scatter | solution.py:194
  238.4 2.0 collective-permute-start
  240.6 29.2 %collective-permute-start.1 = (bf16[256,2048]{1,0:T(8,128)(2,1)S(1)}, bf16[256,2048]{1,0:T(8,128)(2,1)}, u32[]{:S(2)}, u32[]{:S(2)}) collective-permute-start(bf16[256,2048]{1,0:T(8,128)(2,1)S(1)} %maximum_select_fusion.4), channel_id=1, source_target_pairs={{0,2},{1,3},{2,0},{3,1},{4,6},{5,7},{6,4},{7,5},{8,10},{9,11},{10,... | collective-permute-start | bytes 3145736 | tf_op jit(solution)/shard_map/ppermute | solution.py:131
  272.3 73.7 %collective-permute-start.2 = (bf16[512,2048]{1,0:T(8,128)(2,1)S(1)}, bf16[512,2048]{1,0:T(8,128)(2,1)}, u32[]{:S(2)}, u32[]{:S(2)}) collective-permute-start(bf16[512,2048]{1,0:T(8,128)(2,1)S(1)} %maximum_select_fusion.3), channel_id=1, source_target_pairs={{0,4},{1,5},{2,6},{3,7},{4,0},{5,1},{6,2},{7,3},{8,12},{9,13},{10,... | collective-permute-start | bytes 6291464 | tf_op jit(solution)/shard_map/ppermute | solution.py:131
  351.1 111.3 %collective-permute-start.3 = (bf16[1024,2048]{1,0:T(8,128)(2,1)}, bf16[1024,2048]{1,0:T(8,128)(2,1)}, u32[]{:S(2)}, u32[]{:S(2)}) collective-permute-start(bf16[1024,2048]{1,0:T(8,128)(2,1)} %maximum_select_fusion.2), channel_id=1, source_target_pairs={{0,8},{1,9},{2,10},{3,11},{4,12},{5,13},{6,14},{7,15},{8,0},{9,1},... | collective-permute-start | bytes 12582920 | tf_op jit(solution)/shard_map/ppermute | solution.py:131
  352.8 121.5 %copy-start.25 = (s32[1,128,8]{1,2,0:T(8,128)S(1)}, s32[1,128,8]{1,2,0:T(8,128)}, u32[]{:S(2)}) copy-start(s32[1,128,8]{1,2,0:T(8,128)} %param.15) | copy-start | bytes 12292
  472.3 380.5 %collective-permute-start.4 = (bf16[2048,2048]{1,0:T(8,128)(2,1)}, bf16[2048,2048]{1,0:T(8,128)(2,1)}, u32[]{:S(2)}, u32[]{:S(2)}) collective-permute-start(bf16[2048,2048]{1,0:T(8,128)(2,1)} %maximum_select_fusion.1), channel_id=1, source_target_pairs={{0,16},{1,17},{2,18},{3,19},{4,20},{5,21},{6,22},{7,23},{8,24},{9,... | collective-permute-start | bytes 25165832 | tf_op jit(solution)/shard_map/ppermute | solution.py:131
  911.5 15.8 copy-start.5
  1012.3 16.2 copy-start.34
  1056.1 22.3 %copy-start.26 = (s32[1,128,8]{1,2,0:T(8,128)S(1)}, s32[1,128,8]{1,2,0:T(8,128)}, u32[]{:S(2)}) copy-start(s32[1,128,8]{1,2,0:T(8,128)} %param.15) | copy-start | bytes 12292
  1056.1 189.1 %copy-start.1 = (f32[128,2048]{1,0:T(8,128)S(1)}, f32[128,2048]{1,0:T(8,128)}, u32[]{:S(2)}) copy-start(f32[128,2048]{1,0:T(8,128)} %copy-done) | copy-start | bytes 3145732
  1056.1 189.1 %copy-start.22 = (f32[2048]{0:T(1024)S(1)}, f32[2048]{0:T(1024)}, u32[]{:S(2)}) copy-start(f32[2048]{0:T(1024)} %copy-done.21) | copy-start | bytes 24580
  1056.1 189.1 %copy-start.28 = (f32[128]{0:T(128)S(1)}, f32[128]{0:T(128)}, u32[]{:S(2)}) copy-start(f32[128]{0:T(128)} %copy-done.27) | copy-start | bytes 1540
  1056.2 190.8 %copy-start.32 = (f32[128]{0:T(128)S(1)}, f32[128]{0:T(128)}, u32[]{:S(2)}) copy-start(f32[128]{0:T(128)} %copy-done.31) | copy-start | bytes 1540
  1056.2 190.8 %copy-start.10 = (bf16[1,128,2048]{2,1,0:T(8,128)(2,1)S(1)}, bf16[1,128,2048]{2,1,0:T(8,128)(2,1)}, u32[]{:S(2)}) copy-start(bf16[1,128,2048]{2,1,0:T(8,128)(2,1)} %param.14) | copy-start | bytes 1572868
  1058.6 19.8 %all-to-all-start.2 = ((f32[32,2,128]{2,1,0:T(2,128)}), f32[32,2,128]{2,1,0:T(2,128)S(1)}, u32[]{:S(2)}, u32[]{:S(2)}) async-start(f32[32,2,128]{2,1,0:T(2,128)} %get-tuple-element.92), calls=%async_computation.4 | async-start | bytes 65536 | tf_op jit(solution)/shard_map/all_to_all | solution.py:199
  1067.4 254.5 %all-gather.13.cloned.1.call-start = ((), (), s32[]{:S(2)}) async-start(), calls=%async_computation.13 | async-start | bytes 4718592 | tf_op jit(solution)/shard_map/all_gather | solution.py:219
  1248.2 161.4 %reduce-scatter.12.cloned.1.call-start = ((), (), s32[]{:S(2)}) async-start(), calls=%async_computation.15 | async-start | bytes 7864320 | tf_op jit(solution)/shard_map/reduce_scatter | solution.py:238
  1248.7 83.2 %copy-start.12 = (bf16[1024,256]{0,1:T(8,128)(2,1)S(1)}, bf16[1024,256]{0,1:T(8,128)(2,1)}, u32[]{:S(2)}) copy-start(bf16[1024,256]{0,1:T(8,128)(2,1)} %copy-done.11) | copy-start | bytes 1572868
  1321.9 9.9 slice-start
  1326.0 5.9 slice-start.1
  1331.9 1.4 copy-start.16
  1331.9 3.4 copy-start.13
  1331.9 3.4 copy-start.14
  1333.3 3.4 copy-start.7
  1333.3 3.4 copy-start.17
  1335.3 6.6 copy-start.24
  1335.4 6.5 copy-start.30
  1348.6 3.5 copy-start.20
  1352.0 179.5 %reduce-scatter.10.cloned.1.call-start = ((), (), s32[]{:S(2)}) async-start(), calls=%async_computation.14 | async-start | bytes 4718592 | tf_op jit(solution)/shard_map/reduce_scatter | solution.py:233
  1360.1 357.6 %reduce-scatter.6.cloned.1.call-start = ((), (), s32[]{:S(2)}) async-start(), calls=%async_computation.11 | async-start | bytes 17301504 | tf_op jit(solution)/shard_map/reduce_scatter | solution.py:203
  1371.3 381.9 %reduce-scatter.14.cloned.1.call-start = ((), (), s32[]{:S(2)}) async-start(), calls=%async_computation.16 | async-start | bytes 2621440 | tf_op jit(solution)/shard_map/reduce_scatter | solution.py:221
  1372.7 16.9 copy-start.19
  1372.7 16.9 copy-start.33
  1409.6 311.0 %all-to-all-start.3 = ((f32[8,64,768]{2,1,0:T(8,128)}), f32[8,64,768]{2,1,0:T(8,128)}, u32[]{:S(2)}, u32[]{:S(2)}) async-start(f32[8,64,768]{2,1,0:T(8,128)} %bitcast.271), calls=%async_computation.7 | async-start | bytes 3145728 | tf_op jit(solution)/shard_map/all_to_all | solution.py:239
  (6 other events, 6.0 us)
Sparse Core Ops, SparseCore 0:
  44.9 30.1 all-gather.16
  77.2 72.7 all-gather.14
  152.9 78.6 all-gather.8
  238.5 154.4 all-gather.10
  1056.3 188.8 reduce-scatter.7
  1248.3 73.5 all-gather.12
  1352.1 57.3 reduce-scatter.11
  1413.2 118.3 reduce-scatter.9
  1533.9 183.8 reduce-scatter.5
  1720.7 32.4 reduce-scatter.13
